TPU v7x, 32 devices: a whole 2x2x4 slice. The times are simulated.
32 devices in a mesh: heads: 2 (over x), cpo: 4 (over z), cp: 4 (over y, core).
Axes of the slice: x: 2, y: 2, z: 4, core: 2. Of those that a mesh axis runs over, the one named last changes fastest.
Arguments:
- queries: bfloat16 [12, 256, 40, 128], P(None, ('cpo', 'cp'), 'heads'), parts along dimension 2
- attn_out: bfloat16 [12, 256, 40, 128], P(None, ('cpo', 'cp'), 'heads'), parts along dimension 2
- grad_out: bfloat16 [12, 256, 40, 128], P(None, ('cpo', 'cp'), 'heads'), parts along dimension 2
- log_sum_exp: float32 [12, 256, 40], P(None, ('cpo', 'cp'), 'heads'), parts along dimension 2
- key_cache: bfloat16 [19456, 8, 128], P(('cpo', 'cp'), 'heads'), parts along dimension 1
- value_cache: bfloat16 [19456, 8, 128], P(('cpo', 'cp'), 'heads'), parts along dimension 1
Outputs:
- output 1: bfloat16 [12, 256, 40, 128], P(None, ('cpo', 'cp'), 'heads'), parts along dimension 2
- output 2: float32 [19456, 8, 128], P(('cpo', 'cp'), 'heads'), parts along dimension 1
- output 3: float32 [19456, 8, 128], P(('cpo', 'cp'), 'heads'), parts along dimension 1
There are 2 independent parts. A program takes and returns all parts, laid end to end along the dimension named above; each array names one.
All inputs are finite; a program needn't handle non-finite values.
Results may differ from a plain program's by a relative error of at most 0.001.
Values are sent between devices in bfloat16 or wider.
A program may use at most 1 GiB of HBM per device.

v0:
```python
import jax
import jax.numpy as jnp
from jax import lax
from jax.sharding import PartitionSpec as P

CP_AXES = ('cpo', 'cp')


def rows_per_step(n_rows, row_width):
    block_rows = n_rows
    while block_rows % 2 == 0 and block_rows * row_width > 4194304:
        block_rows = block_rows // 2
    return block_rows


def make_step(key_part, value_part, key_pos, softmax_scale):
    def block_step(carry_acc, operand):
        acc_key, acc_value = carry_acc
        q_blk, g_blk, stat_blk, row_start = operand
        lse_rows = jnp.transpose(stat_blk[..., 0], (1, 0, 2))
        delta_rows = jnp.transpose(stat_blk[..., 1], (1, 0, 2))
        scores = jnp.einsum('rhgd,khd->hrgk', q_blk, key_part, preferred_element_type=jnp.float32)
        q_pos = row_start + jnp.arange(q_blk.shape[0])
        visible = (key_pos[None, :] <= q_pos[:, None])[None, :, None, :]
        attn_prob = jnp.where(visible, jnp.exp(scores * softmax_scale - lse_rows[..., None]), 0.0)
        acc_value = acc_value + jnp.einsum('hrgk,rhgd->hkd', attn_prob.astype(jnp.bfloat16), g_blk, preferred_element_type=jnp.float32)
        grad_prob = jnp.einsum('rhgd,khd->hrgk', g_blk, value_part, preferred_element_type=jnp.float32)
        grad_scores = (attn_prob * (grad_prob - delta_rows[..., None])).astype(jnp.bfloat16)
        dq_blk = jnp.einsum('hrgk,khd->rhgd', grad_scores, key_part, preferred_element_type=jnp.float32) * softmax_scale
        acc_key = acc_key + softmax_scale * jnp.einsum('hrgk,rhgd->hkd', grad_scores, q_blk, preferred_element_type=jnp.float32)
        return (acc_key, acc_value), dq_blk

    return block_step


def solution(mesh):
    n_dev = mesh.shape['cpo'] * mesh.shape['cp']
    inner_size = mesh.shape['cp']
    row_spec = P(None, CP_AXES, 'heads', None)
    stat_spec = P(None, CP_AXES, 'heads')
    key_spec = P(CP_AXES, 'heads', None)

    def local_grads(queries, attn_out, grad_out, log_sum_exp, key_cache, value_cache):
        n_slices, rows_dev, q_heads, head_dim = queries.shape
        key_rows = key_cache.shape[0]
        kv_heads = key_cache.shape[1]
        group_size = q_heads // kv_heads
        slice_len = rows_dev * n_dev
        prefix_base = key_rows * n_dev - n_slices * slice_len
        softmax_scale = head_dim ** -0.5
        dev_idx = lax.axis_index('cpo') * inner_size + lax.axis_index('cp')
        key_pos = dev_idx * key_rows + jnp.arange(key_rows)
        block_rows = rows_per_step(slice_len, q_heads * key_rows)
        n_blocks = slice_len // block_rows
        blk_shape = (n_blocks, block_rows, kv_heads, group_size)
        row_delta = jnp.sum(grad_out.astype(jnp.float32) * attn_out.astype(jnp.float32), axis=-1)
        row_stats = jnp.stack([log_sum_exp, row_delta], axis=-1)
        block_step = make_step(key_cache, value_cache, key_pos, softmax_scale)
        acc_key = jnp.zeros((kv_heads, key_rows, head_dim), jnp.float32)
        acc_value = jnp.zeros((kv_heads, key_rows, head_dim), jnp.float32)
        dq_list = []
        for slice_idx in reversed(range(n_slices)):
            q_all = lax.all_gather(queries[slice_idx], CP_AXES, axis=0, tiled=True)
            g_all = lax.all_gather(grad_out[slice_idx], CP_AXES, axis=0, tiled=True)
            stat_all = lax.all_gather(row_stats[slice_idx], CP_AXES, axis=0, tiled=True)
            row_starts = prefix_base + slice_idx * slice_len + block_rows * jnp.arange(n_blocks)
            operands = (q_all.reshape(blk_shape + (head_dim,)), g_all.reshape(blk_shape + (head_dim,)), stat_all.reshape(blk_shape + (2,)), row_starts)
            (acc_key, acc_value), dq_blocks = lax.scan(block_step, (acc_key, acc_value), operands)
            dq_part = dq_blocks.reshape(slice_len, q_heads, head_dim)
            dq_list.append(lax.psum_scatter(dq_part, CP_AXES, scatter_dimension=0, tiled=True).astype(jnp.bfloat16))
        grad_query = jnp.stack(dq_list[::-1])
        return grad_query, jnp.transpose(acc_key, (1, 0, 2)), jnp.transpose(acc_value, (1, 0, 2))

    return jax.shard_map(local_grads, mesh=mesh, in_specs=(row_spec, row_spec, row_spec, stat_spec, key_spec, key_spec), out_specs=(row_spec, key_spec, key_spec), check_vma=False)
```

profile of v0, /device:TPU:0, one launch (start us, length us, event | category | flops | bytes accessed | tf_op | source)
XLA Modules:
  0.0 1832.2 jit_solution(7081046863001082617)
XLA Ops:
  38.7 23.8 %all-gather.1 = f32[1,256,20,2]{2,3,0,1:T(2,128)S(1)} all-gather(f32[1,16,20,2]{2,3,0,1:T(2,128)S(1)} %copy.221), channel_id=3, replica_groups=mesh['heads'=2,'cpo'=4,'cp'=4] {'cpo','cp'}, dimensions={1}, use_global_device_ids=true | all-gather | bytes 43520 | tf_op jit(solution)/shard_map/all_gather | solution.py:65
  65.3 18.5 %all-gather.4 = f32[1,256,20,2]{2,3,0,1:T(2,128)S(1)} all-gather(f32[1,16,20,2]{2,3,0,1:T(2,128)S(1)} %copy.228), channel_id=6, replica_groups=mesh['heads'=2,'cpo'=4,'cp'=4] {'cpo','cp'}, dimensions={1}, use_global_device_ids=true | all-gather | bytes 43520 | tf_op jit(solution)/shard_map/all_gather | solution.py:65
  84.6 19.5 %all-gather.7 = f32[1,256,20,2]{2,3,0,1:T(2,128)S(1)} all-gather(f32[1,16,20,2]{2,3,0,1:T(2,128)S(1)} %copy.235), channel_id=9, replica_groups=mesh['heads'=2,'cpo'=4,'cp'=4] {'cpo','cp'}, dimensions={1}, use_global_device_ids=true | all-gather | bytes 43520 | tf_op jit(solution)/shard_map/all_gather | solution.py:65
  105.0 18.5 %all-gather.10 = f32[1,256,20,2]{2,3,0,1:T(2,128)S(1)} all-gather(f32[1,16,20,2]{2,3,0,1:T(2,128)S(1)} %copy.242), channel_id=12, replica_groups=mesh['heads'=2,'cpo'=4,'cp'=4] {'cpo','cp'}, dimensions={1}, use_global_device_ids=true | all-gather | bytes 43520 | tf_op jit(solution)/shard_map/all_gather | solution.py:65
  124.4 19.4 %all-gather.13 = f32[1,256,20,2]{2,3,0,1:T(2,128)S(1)} all-gather(f32[1,16,20,2]{2,3,0,1:T(2,128)S(1)} %copy.249), channel_id=15, replica_groups=mesh['heads'=2,'cpo'=4,'cp'=4] {'cpo','cp'}, dimensions={1}, use_global_device_ids=true | all-gather | bytes 43520 | tf_op jit(solution)/shard_map/all_gather | solution.py:65
  144.7 18.5 %all-gather.16 = f32[1,256,20,2]{2,3,0,1:T(2,128)S(1)} all-gather(f32[1,16,20,2]{2,3,0,1:T(2,128)S(1)} %copy.256), channel_id=18, replica_groups=mesh['heads'=2,'cpo'=4,'cp'=4] {'cpo','cp'}, dimensions={1}, use_global_device_ids=true | all-gather | bytes 43520 | tf_op jit(solution)/shard_map/all_gather | solution.py:65
  164.1 19.4 %all-gather.19 = f32[1,256,20,2]{2,3,0,1:T(2,128)S(1)} all-gather(f32[1,16,20,2]{2,3,0,1:T(2,128)S(1)} %copy.263), channel_id=21, replica_groups=mesh['heads'=2,'cpo'=4,'cp'=4] {'cpo','cp'}, dimensions={1}, use_global_device_ids=true | all-gather | bytes 43520 | tf_op jit(solution)/shard_map/all_gather | solution.py:65
  184.4 18.2 all-gather.22
  203.5 19.5 %all-gather.25 = f32[1,256,20,2]{2,3,0,1:T(2,128)S(1)} all-gather(f32[1,16,20,2]{2,3,0,1:T(2,128)S(1)} %copy.277), channel_id=27, replica_groups=mesh['heads'=2,'cpo'=4,'cp'=4] {'cpo','cp'}, dimensions={1}, use_global_device_ids=true | all-gather | bytes 43520 | tf_op jit(solution)/shard_map/all_gather | solution.py:65
  224.0 18.6 %all-gather.28 = f32[1,256,20,2]{2,3,0,1:T(2,128)S(1)} all-gather(f32[1,16,20,2]{2,3,0,1:T(2,128)S(1)} %copy.284), channel_id=30, replica_groups=mesh['heads'=2,'cpo'=4,'cp'=4] {'cpo','cp'}, dimensions={1}, use_global_device_ids=true | all-gather | bytes 43520 | tf_op jit(solution)/shard_map/all_gather | solution.py:65
  243.5 19.5 %all-gather.31 = f32[1,256,20,2]{2,3,0,1:T(2,128)S(1)} all-gather(f32[1,16,20,2]{2,3,0,1:T(2,128)S(1)} %copy.291), channel_id=33, replica_groups=mesh['heads'=2,'cpo'=4,'cp'=4] {'cpo','cp'}, dimensions={1}, use_global_device_ids=true | all-gather | bytes 43520 | tf_op jit(solution)/shard_map/all_gather | solution.py:65
  263.8 19.1 %all-gather.34 = f32[1,256,20,2]{2,3,0,1:T(2,128)S(1)} all-gather(f32[1,16,20,2]{2,3,0,1:T(2,128)S(1)} %copy.298), channel_id=36, replica_groups=mesh['heads'=2,'cpo'=4,'cp'=4] {'cpo','cp'}, dimensions={1}, use_global_device_ids=true | all-gather | bytes 43520 | tf_op jit(solution)/shard_map/all_gather | solution.py:65
  285.6 53.2 %while.191 = (s32[]{:T(128)}, f32[4,1216,128]{2,1,0:T(8,128)S(1)}, f32[4,1216,128]{2,1,0:T(8,128)}, f32[2,128,4,5,128]{4,1,0,3,2:T(8,128)}, s32[2]{0:T(128)S(1)}...) while((s32[]{:T(128)}, f32[4,1216,128]{2,1,0:T(8,128)S(1)}, ...), condition=%wide.region_2.3_spmd.clone, body=%wide.region_1.2_spmd.clone.sunk | while | flops 4019315968 | bytes 204139536 | solution.py:68
  340.6 58.8 %while.180 = (s32[]{:T(128)}, f32[4,1216,128]{2,1,0:T(8,128)S(1)}, f32[4,1216,128]{2,1,0:T(8,128)}, f32[2,128,4,5,128]{4,1,0,3,2:T(8,128)}, s32[2]{0:T(128)S(1)}...) while((s32[]{:T(128)}, f32[4,1216,128]{2,1,0:T(8,128)S(1)}, ...), condition=%wide.region_4.5_spmd.clone, body=%wide.region_3.4_spmd.clone.sunk | while | flops 4018070784 | bytes 84517608 | solution.py:68
  345.7 8.1 multiply_convert_fusion.24
  375.0 8.1 multiply_convert_fusion.24
  401.4 58.8 %while.181 = (s32[]{:T(128)}, f32[4,1216,128]{2,1,0:T(8,128)S(1)}, f32[4,1216,128]{2,1,0:T(8,128)}, f32[2,128,4,5,128]{4,1,0,3,2:T(8,128)}, s32[2]{0:T(128)S(1)}...) while((s32[]{:T(128)}, f32[4,1216,128]{2,1,0:T(8,128)S(1)}, ...), condition=%wide.region_6.7_spmd.clone, body=%wide.region_5.6_spmd.clone.sunk | while | flops 4018070784 | bytes 84517608 | solution.py:68
  435.7 8.1 multiply_convert_fusion.25
  462.2 59.1 %while.182 = (s32[]{:T(128)}, f32[4,1216,128]{2,1,0:T(8,128)S(1)}, f32[4,1216,128]{2,1,0:T(8,128)}, f32[2,128,4,5,128]{4,1,0,3,2:T(8,128)}, s32[2]{0:T(128)S(1)}...) while((s32[]{:T(128)}, f32[4,1216,128]{2,1,0:T(8,128)S(1)}, ...), condition=%wide.region_8.9_spmd.clone, body=%wide.region_7.8_spmd.clone.sunk | while | flops 4018070784 | bytes 84517608 | solution.py:68
  523.1 58.8 %while.183 = (s32[]{:T(128)}, f32[4,1216,128]{2,1,0:T(8,128)S(1)}, f32[4,1216,128]{2,1,0:T(8,128)}, f32[2,128,4,5,128]{4,1,0,3,2:T(8,128)}, s32[2]{0:T(128)S(1)}...) while((s32[]{:T(128)}, f32[4,1216,128]{2,1,0:T(8,128)S(1)}, ...), condition=%wide.region_10.11_spmd.clone, body=%wide.region_9.10_spmd.clone.sunk | while | flops 4018070784 | bytes 84517608 | solution.py:68
  528.2 8.1 multiply_convert_fusion.27
  583.7 58.8 %while.184 = (s32[]{:T(128)}, f32[4,1216,128]{2,1,0:T(8,128)S(1)}, f32[4,1216,128]{2,1,0:T(8,128)}, f32[2,128,4,5,128]{4,1,0,3,2:T(8,128)}, s32[2]{0:T(128)S(1)}...) while((s32[]{:T(128)}, f32[4,1216,128]{2,1,0:T(8,128)S(1)}, ...), condition=%wide.region_12.13_spmd.clone, body=%wide.region_11.12_spmd.clone.sunk | while | flops 4018070784 | bytes 84517608 | solution.py:68
  588.8 8.1 multiply_convert_fusion.28
  644.4 59.0 %while.185 = (s32[]{:T(128)}, f32[4,1216,128]{2,1,0:T(8,128)S(1)}, f32[4,1216,128]{2,1,0:T(8,128)}, f32[2,128,4,5,128]{4,1,0,3,2:T(8,128)}, s32[2]{0:T(128)S(1)}...) while((s32[]{:T(128)}, f32[4,1216,128]{2,1,0:T(8,128)S(1)}, ...), condition=%wide.region_14.15_spmd.clone, body=%wide.region_13.14_spmd.clone.sunk | while | flops 4018070784 | bytes 84517608 | solution.py:68
  705.3 58.8 %while.186 = (s32[]{:T(128)}, f32[4,1216,128]{2,1,0:T(8,128)S(1)}, f32[4,1216,128]{2,1,0:T(8,128)}, f32[2,128,4,5,128]{4,1,0,3,2:T(8,128)}, s32[2]{0:T(128)S(1)}...) while((s32[]{:T(128)}, f32[4,1216,128]{2,1,0:T(8,128)S(1)}, ...), condition=%wide.region_16.17_spmd.clone, body=%wide.region_15.16_spmd.clone.sunk | while | flops 4018070784 | bytes 84517608 | solution.py:68
  739.6 8.1 multiply_convert_fusion.30
  766.0 58.9 %while.187 = (s32[]{:T(128)}, f32[4,1216,128]{2,1,0:T(8,128)S(1)}, f32[4,1216,128]{2,1,0:T(8,128)}, f32[2,128,4,5,128]{4,1,0,3,2:T(8,128)}, s32[2]{0:T(128)S(1)}...) while((s32[]{:T(128)}, f32[4,1216,128]{2,1,0:T(8,128)S(1)}, ...), condition=%wide.region_18.19_spmd.clone, body=%wide.region_17.18_spmd.clone.sunk | while | flops 4018070784 | bytes 84517608 | solution.py:68
  771.0 8.1 multiply_convert_fusion.31
  800.3 8.1 multiply_convert_fusion.31
  826.7 59.0 %while.188 = (s32[]{:T(128)}, f32[4,1216,128]{2,1,0:T(8,128)S(1)}, f32[4,1216,128]{2,1,0:T(8,128)}, f32[2,128,4,5,128]{4,1,0,3,2:T(8,128)}, s32[2]{0:T(128)S(1)}...) while((s32[]{:T(128)}, f32[4,1216,128]{2,1,0:T(8,128)S(1)}, ...), condition=%wide.region_20.21_spmd.clone, body=%wide.region_19.20_spmd.clone.sunk | while | flops 4018070784 | bytes 84517608 | solution.py:68
  887.5 58.7 %while.189 = (s32[]{:T(128)}, f32[4,1216,128]{2,1,0:T(8,128)S(1)}, f32[4,1216,128]{2,1,0:T(8,128)}, f32[2,128,4,5,128]{4,1,0,3,2:T(8,128)}, s32[2]{0:T(128)S(1)}...) while((s32[]{:T(128)}, f32[4,1216,128]{2,1,0:T(8,128)S(1)}, ...), condition=%wide.region_22.23_spmd.clone, body=%wide.region_21.22_spmd.clone.sunk | while | flops 4018070784 | bytes 84517608 | solution.py:68
  921.8 8.1 multiply_convert_fusion.33
  946.3 16.5 all-gather.107.cloned.1.call-done
  964.5 58.8 %while.190 = (s32[]{:T(128)}, f32[4,1216,128]{2,1,0:T(8,128)S(1)}, f32[4,1216,128]{2,1,0:T(8,128)}, f32[2,128,4,5,128]{4,1,0,3,2:T(8,128)}, s32[2]{0:T(128)S(1)}...) while((s32[]{:T(128)}, f32[4,1216,128]{2,1,0:T(8,128)S(1)}, ...), condition=%wide.region_24.25_spmd.clone, body=%wide.region_23.24_spmd.clone.sunk | while | flops 4018070784 | bytes 84517608 | solution.py:68
  969.6 8.1 multiply_convert_fusion.34
  1030.7 12.8 copy_bitcast_fusion.12
  1043.5 44.2 %reduce-scatter.13.cloned.1.call-done = f32[16,20,128]{2,0,1:T(8,128)} async-done(((f32[256,20,128]{2,0,1:T(8,128)}), f32[16,20,128]{2,0,1:T(8,128)}) %reduce-scatter.13.cloned.1.call-update) | async-done | bytes 163856 | tf_op jit(solution)/shard_map/reduce_scatter | solution.py:70
  1088.7 65.9 %reduce-scatter.15.cloned.1.call-done = f32[16,20,128]{2,0,1:T(8,128)} async-done(((f32[256,20,128]{2,0,1:T(8,128)}), f32[16,20,128]{2,0,1:T(8,128)}) %reduce-scatter.15.cloned.1.call-update) | async-done | bytes 163856 | tf_op jit(solution)/shard_map/reduce_scatter | solution.py:70
  1155.5 65.9 %reduce-scatter.17.cloned.1.call-done = f32[16,20,128]{2,0,1:T(8,128)} async-done(((f32[256,20,128]{2,0,1:T(8,128)}), f32[16,20,128]{2,0,1:T(8,128)}) %reduce-scatter.17.cloned.1.call-update) | async-done | bytes 163856 | tf_op jit(solution)/shard_map/reduce_scatter | solution.py:70
  1222.3 66.0 %reduce-scatter.19.cloned.1.call-done = f32[16,20,128]{2,0,1:T(8,128)} async-done(((f32[256,20,128]{2,0,1:T(8,128)}), f32[16,20,128]{2,0,1:T(8,128)}) %reduce-scatter.19.cloned.1.call-update) | async-done | bytes 163856 | tf_op jit(solution)/shard_map/reduce_scatter | solution.py:70
  1289.2 66.0 %reduce-scatter.21.cloned.1.call-done = f32[16,20,128]{2,0,1:T(8,128)} async-done(((f32[256,20,128]{2,0,1:T(8,128)}), f32[16,20,128]{2,0,1:T(8,128)}) %reduce-scatter.21.cloned.1.call-update) | async-done | bytes 163856 | tf_op jit(solution)/shard_map/reduce_scatter | solution.py:70
  1356.2 65.9 %reduce-scatter.23.cloned.1.call-done = f32[16,20,128]{2,0,1:T(8,128)} async-done(((f32[256,20,128]{2,0,1:T(8,128)}), f32[16,20,128]{2,0,1:T(8,128)}) %reduce-scatter.23.cloned.1.call-update) | async-done | bytes 163856 | tf_op jit(solution)/shard_map/reduce_scatter | solution.py:70
  1423.0 65.9 %reduce-scatter.25.cloned.1.call-done = f32[16,20,128]{2,0,1:T(8,128)} async-done(((f32[256,20,128]{2,0,1:T(8,128)}), f32[16,20,128]{2,0,1:T(8,128)}) %reduce-scatter.25.cloned.1.call-update) | async-done | bytes 163856 | tf_op jit(solution)/shard_map/reduce_scatter | solution.py:70
  1489.8 66.0 %reduce-scatter.27.cloned.1.call-done = f32[16,20,128]{2,0,1:T(8,128)} async-done(((f32[256,20,128]{2,0,1:T(8,128)}), f32[16,20,128]{2,0,1:T(8,128)}) %reduce-scatter.27.cloned.1.call-update) | async-done | bytes 163856 | tf_op jit(solution)/shard_map/reduce_scatter | solution.py:70
  1556.7 65.9 %reduce-scatter.29.cloned.1.call-done = f32[16,20,128]{2,0,1:T(8,128)} async-done(((f32[256,20,128]{2,0,1:T(8,128)}), f32[16,20,128]{2,0,1:T(8,128)}) %reduce-scatter.29.cloned.1.call-update) | async-done | bytes 163856 | tf_op jit(solution)/shard_map/reduce_scatter | solution.py:70
  1623.5 66.0 %reduce-scatter.31.cloned.1.call-done = f32[16,20,128]{2,0,1:T(8,128)} async-done(((f32[256,20,128]{2,0,1:T(8,128)}), f32[16,20,128]{2,0,1:T(8,128)}) %reduce-scatter.31.cloned.1.call-update) | async-done | bytes 163856 | tf_op jit(solution)/shard_map/reduce_scatter | solution.py:70
  1690.5 66.0 %reduce-scatter.33.cloned.1.call-done = f32[16,20,128]{2,0,1:T(8,128)} async-done(((f32[256,20,128]{2,0,1:T(8,128)}), f32[16,20,128]{2,0,1:T(8,128)}) %reduce-scatter.33.cloned.1.call-update) | async-done | bytes 163856 | tf_op jit(solution)/shard_map/reduce_scatter | solution.py:70
  1757.4 66.0 %reduce-scatter.35.cloned.1.call-done = f32[16,20,128]{2,0,1:T(8,128)} async-done(((f32[256,20,128]{2,0,1:T(8,128)}), f32[16,20,128]{2,0,1:T(8,128)}) %reduce-scatter.35.cloned.1.call-update) | async-done | bytes 163856 | tf_op jit(solution)/shard_map/reduce_scatter | solution.py:70
  (637 shorter events, 699.9 us)
Async XLA Ops:
  7.2 276.6 %all-gather.61.cloned.1.call-start = ((), (), s32[]{:S(2)}) async-start(), calls=%async_computation.24 | async-start | bytes 1392640 | tf_op jit(solution)/shard_map/all_gather | solution.py:63
  9.5 274.2 %all-gather.63.cloned.1.call-start = ((), (), s32[]{:S(2)}) async-start(), calls=%async_computation.25 | async-start | bytes 1392640 | tf_op jit(solution)/shard_map/all_gather | solution.py:64
  10.6 328.2 %all-gather.65.cloned.1.call-start = ((), (), s32[]{:S(2)}) async-start(), calls=%async_computation.26 | async-start | bytes 1392640 | tf_op jit(solution)/shard_map/all_gather | solution.py:63
  11.3 327.5 %all-gather.67.cloned.1.call-start = ((), (), s32[]{:S(2)}) async-start(), calls=%async_computation.27 | async-start | bytes 1392640 | tf_op jit(solution)/shard_map/all_gather | solution.py:64
  11.9 387.6 %all-gather.69.cloned.1.call-start = ((), (), s32[]{:S(2)}) async-start(), calls=%async_computation.28 | async-start | bytes 1392640 | tf_op jit(solution)/shard_map/all_gather | solution.py:63
  12.5 387.0 %all-gather.71.cloned.1.call-start = ((), (), s32[]{:S(2)}) async-start(), calls=%async_computation.29 | async-start | bytes 1392640 | tf_op jit(solution)/shard_map/all_gather | solution.py:64
  13.0 447.2 %all-gather.73.cloned.1.call-start = ((), (), s32[]{:S(2)}) async-start(), calls=%async_computation.30 | async-start | bytes 1392640 | tf_op jit(solution)/shard_map/all_gather | solution.py:63
  13.8 446.5 %all-gather.75.cloned.1.call-start = ((), (), s32[]{:S(2)}) async-start(), calls=%async_computation.31 | async-start | bytes 1392640 | tf_op jit(solution)/shard_map/all_gather | solution.py:64
  14.5 506.8 %all-gather.77.cloned.1.call-start = ((), (), s32[]{:S(2)}) async-start(), calls=%async_computation.32 | async-start | bytes 1392640 | tf_op jit(solution)/shard_map/all_gather | solution.py:63
  15.3 506.1 %all-gather.79.cloned.1.call-start = ((), (), s32[]{:S(2)}) async-start(), calls=%async_computation.33 | async-start | bytes 1392640 | tf_op jit(solution)/shard_map/all_gather | solution.py:64
  15.9 566.0 %all-gather.81.cloned.1.call-start = ((), (), s32[]{:S(2)}) async-start(), calls=%async_computation.34 | async-start | bytes 1392640 | tf_op jit(solution)/shard_map/all_gather | solution.py:63
  16.6 565.3 %all-gather.83.cloned.1.call-start = ((), (), s32[]{:S(2)}) async-start(), calls=%async_computation.35 | async-start | bytes 1392640 | tf_op jit(solution)/shard_map/all_gather | solution.py:64
  17.2 625.4 %all-gather.85.cloned.1.call-start = ((), (), s32[]{:S(2)}) async-start(), calls=%async_computation.36 | async-start | bytes 1392640 | tf_op jit(solution)/shard_map/all_gather | solution.py:63
  17.9 624.6 %all-gather.87.cloned.1.call-start = ((), (), s32[]{:S(2)}) async-start(), calls=%async_computation.37 | async-start | bytes 1392640 | tf_op jit(solution)/shard_map/all_gather | solution.py:64
  18.5 685.0 %all-gather.89.cloned.1.call-start = ((), (), s32[]{:S(2)}) async-start(), calls=%async_computation.38 | async-start | bytes 1392640 | tf_op jit(solution)/shard_map/all_gather | solution.py:63
  19.1 684.4 %all-gather.91.cloned.1.call-start = ((), (), s32[]{:S(2)}) async-start(), calls=%async_computation.39 | async-start | bytes 1392640 | tf_op jit(solution)/shard_map/all_gather | solution.py:64
  19.7 744.4 %all-gather.93.cloned.1.call-start = ((), (), s32[]{:S(2)}) async-start(), calls=%async_computation.40 | async-start | bytes 1392640 | tf_op jit(solution)/shard_map/all_gather | solution.py:63
  20.2 743.9 %all-gather.95.cloned.1.call-start = ((), (), s32[]{:S(2)}) async-start(), calls=%async_computation.41 | async-start | bytes 1392640 | tf_op jit(solution)/shard_map/all_gather | solution.py:64
  20.8 804.0 %all-gather.97.cloned.1.call-start = ((), (), s32[]{:S(2)}) async-start(), calls=%async_computation.42 | async-start | bytes 1392640 | tf_op jit(solution)/shard_map/all_gather | solution.py:63
  21.6 803.3 %all-gather.99.cloned.1.call-start = ((), (), s32[]{:S(2)}) async-start(), calls=%async_computation.43 | async-start | bytes 1392640 | tf_op jit(solution)/shard_map/all_gather | solution.py:64
  22.2 863.5 %all-gather.101.cloned.1.call-start = ((), (), s32[]{:S(2)}) async-start(), calls=%async_computation.44 | async-start | bytes 1392640 | tf_op jit(solution)/shard_map/all_gather | solution.py:63
  22.9 862.8 %all-gather.103.cloned.1.call-start = ((), (), s32[]{:S(2)}) async-start(), calls=%async_computation.45 | async-start | bytes 1392640 | tf_op jit(solution)/shard_map/all_gather | solution.py:64
  23.6 922.6 %all-gather.105.cloned.1.call-start = ((), (), s32[]{:S(2)}) async-start(), calls=%async_computation.46 | async-start | bytes 1392640 | tf_op jit(solution)/shard_map/all_gather | solution.py:63
  24.4 938.4 %all-gather.107.cloned.1.call-start = ((), (), s32[]{:S(2)}) async-start(), calls=%async_computation.47 | async-start | bytes 1392640 | tf_op jit(solution)/shard_map/all_gather | solution.py:64
  25.0 1062.8 %reduce-scatter.13.cloned.1.call-start = ((), (), s32[]{:S(2)}) async-start(), calls=%async_computation.12 | async-start | bytes 2785280 | tf_op jit(solution)/shard_map/reduce_scatter | solution.py:70
  296.4 11.6 slice-start
  323.0 11.6 slice-start
  435.7 8.2 copy-start.22
  528.1 8.2 copy-start.20
  588.8 8.2 copy-start.19
  739.6 8.2 copy-start.17
  771.0 8.2 copy-start.16
  800.3 8.2 copy-start.16
  921.8 8.2 copy-start.14
  946.3 18.3 copy-start.30
  946.3 18.3 copy-start.44
  969.6 8.2 copy-start.13
  1023.4 131.2 %reduce-scatter.15.cloned.1.call-start = ((), (), s32[]{:S(2)}) async-start(), calls=%async_computation.13 | async-start | bytes 2785280 | tf_op jit(solution)/shard_map/reduce_scatter | solution.py:70
  1024.0 197.4 %reduce-scatter.17.cloned.1.call-start = ((), (), s32[]{:S(2)}) async-start(), calls=%async_computation.14 | async-start | bytes 2785280 | tf_op jit(solution)/shard_map/reduce_scatter | solution.py:70
  1024.5 263.7 %reduce-scatter.19.cloned.1.call-start = ((), (), s32[]{:S(2)}) async-start(), calls=%async_computation.15 | async-start | bytes 2785280 | tf_op jit(solution)/shard_map/reduce_scatter | solution.py:70
  1025.3 329.9 %reduce-scatter.21.cloned.1.call-start = ((), (), s32[]{:S(2)}) async-start(), calls=%async_computation.16 | async-start | bytes 2785280 | tf_op jit(solution)/shard_map/reduce_scatter | solution.py:70
  1026.0 396.0 %reduce-scatter.23.cloned.1.call-start = ((), (), s32[]{:S(2)}) async-start(), calls=%async_computation.17 | async-start | bytes 2785280 | tf_op jit(solution)/shard_map/reduce_scatter | solution.py:70
  1026.6 462.2 %reduce-scatter.25.cloned.1.call-start = ((), (), s32[]{:S(2)}) async-start(), calls=%async_computation.18 | async-start | bytes 2785280 | tf_op jit(solution)/shard_map/reduce_scatter | solution.py:70
  1027.3 528.4 %reduce-scatter.27.cloned.1.call-start = ((), (), s32[]{:S(2)}) async-start(), calls=%async_computation.19 | async-start | bytes 2785280 | tf_op jit(solution)/shard_map/reduce_scatter | solution.py:70
  1028.1 594.5 %reduce-scatter.29.cloned.1.call-start = ((), (), s32[]{:S(2)}) async-start(), calls=%async_computation.20 | async-start | bytes 2785280 | tf_op jit(solution)/shard_map/reduce_scatter | solution.py:70
  1028.7 660.9 %reduce-scatter.31.cloned.1.call-start = ((), (), s32[]{:S(2)}) async-start(), calls=%async_computation.21 | async-start | bytes 2785280 | tf_op jit(solution)/shard_map/reduce_scatter | solution.py:70
  1029.4 727.1 %reduce-scatter.33.cloned.1.call-start = ((), (), s32[]{:S(2)}) async-start(), calls=%async_computation.22 | async-start | bytes 2785280 | tf_op jit(solution)/shard_map/reduce_scatter | solution.py:70
  1030.2 793.2 %reduce-scatter.35.cloned.1.call-start = ((), (), s32[]{:S(2)}) async-start(), calls=%async_computation.23 | async-start | bytes 2785280 | tf_op jit(solution)/shard_map/reduce_scatter | solution.py:70
  (78 other events, 370.8 us)
Sparse Core Ops, SparseCore 0:
  10.1 40.3 all-gather.60
  52.7 37.7 all-gather.62
  92.6 37.2 all-gather.64
  131.9 37.1 all-gather.66
  171.1 37.3 all-gather.68
  210.6 37.1 all-gather.70
  249.9 37.7 all-gather.72
  289.9 37.8 all-gather.74
  330.0 37.3 all-gather.76
  369.4 37.6 all-gather.78
  409.2 37.5 all-gather.80
  448.8 37.5 all-gather.82
  488.6 37.6 all-gather.84
  528.3 37.5 all-gather.86
  567.9 37.5 all-gather.88
  607.5 37.5 all-gather.90
  647.1 37.5 all-gather.92
  686.7 37.5 all-gather.94
  726.5 37.5 all-gather.96
  766.1 37.5 all-gather.98
  805.9 37.6 all-gather.100
  845.7 37.5 all-gather.102
  885.5 37.5 all-gather.104
  925.1 37.5 all-gather.106
  1023.5 64.2 reduce-scatter.12
  1091.4 63.1 reduce-scatter.14
  1158.1 63.1 reduce-scatter.16
  1225.1 63.1 reduce-scatter.18
  1292.1 63.1 reduce-scatter.20
  1358.8 63.1 reduce-scatter.22
  1425.8 62.9 reduce-scatter.24
  1492.6 63.1 reduce-scatter.26
  1559.4 63.1 reduce-scatter.28
  1626.4 63.1 reduce-scatter.30
  1693.3 63.1 reduce-scatter.32
  1760.1 63.2 reduce-scatter.34
where the time goes:
time: 1840 us; the launch traced here: 1830 us
  waiting for transfers between devices  806 us (44%)
  matrix products  656 us (36%)
  blocking collectives  233 us (13%)
  local copies, waits for them, and re-layouts  73.9 us (4%)
  other arithmetic  42.3 us (2%)
    reduce_scatter x12, waiting for transfers between devices, local_grads(): lax.psum_scatter(dq_part, CP_AXES, scatter_dimension=0, tiled=True)  770 us
    all_gather x12, blocking collectives, local_grads(): stat_all = lax.all_gather(row_stats[slice_idx], CP_AXES, axis=0, tiled=True)  233 us
    dot_general x24, matrix products, block_step(): jnp.einsum('rhgd,khd->hrgk', g_blk, value_part, preferred_element_type=jn...  191 us
    dot_general x24, matrix products, block_step(): jnp.einsum('hrgk,khd->rhgd', grad_scores, key_part, preferred_element_typ...  142 us
    dot_general x24, matrix products, block_step(): jnp.einsum('hrgk,rhgd->hkd', attn_prob.astype(jnp.bfloat16), g_blk, prefe...  125 us
    dot_general x24, matrix products, block_step(): jnp.einsum('hrgk,rhgd->hkd', grad_scores, q_blk, preferred_element_type=j...  120 us
    dot_general x24, matrix products, block_step(): jnp.einsum('rhgd,khd->hrgk', q_blk, key_part, preferred_element_type=jnp....  79.1 us
  transfers between devices with their start and end apart: 36, of which 13 were waited for; matrix products, arithmetic and copies ran while one was open for 38% of the time, Pallas kernels for 0%

commit v1 on v0

v1 whole, which is shorter than its diff:
```python
import functools

import jax
import jax.numpy as jnp
from jax import lax
from jax.experimental import pallas as pl
from jax.experimental.pallas import tpu as pltpu
from jax.sharding import PartitionSpec as P

CP_AXES = ('cpo', 'cp')
MESH = pl.DeviceIdType.MESH
LOG2E = 1.4426950408889634
KEY_BLOCK = 256
SUB = 256
AHEAD = 4
FIRST = 2


def attention_kernel(n_pl, n_cp, n_pref_last, scale, *refs):
    (qg, kv, st, qpos, dq_out, dk_out, dv_out) = refs[:7]
    (gat, kv_scr, kt_scr, vt_scr, st_scr, dqp, ru, rd, dqb, dk_scr, dv_scr, dko, dvo, qt_scr, gt_scr, l_scr, d_scr) = refs[7:24]
    (q_s, q_r, kv_s, kv_r, st_s, st_r, sz_s, sz_r, ag_s, ag_r, rs_s, rs_r, dq_s, dq_r, dk_s, dk_r) = refs[24:]
    n_slices = gat.shape[0]
    rows = gat.shape[2]
    piece = rows // n_pl
    part = piece // n_cp
    key_rows = kv.shape[2]
    n_blocks = kv_scr.shape[1] // KEY_BLOCK
    far = n_pl - 1
    z = lax.axis_index('cpo')
    c = lax.axis_index('cp')

    def mate(s):
        return {0: c, 1: c + 1 - 2 * lax.rem(c, 2), 2: lax.rem(c + 2, n_cp), 3: n_cp - 1 - c}[s]

    def remote(src, dst, send, recv, **where):
        return pltpu.make_async_remote_copy(src_ref=src, dst_ref=dst, send_sem=send, recv_sem=recv, device_id=where, device_id_type=MESH)

    def slot(k):
        return pl.ds(k * piece, piece)

    barrier = pltpu.get_barrier_semaphore()
    for s in range(1, n_cp):
        pl.semaphore_signal(barrier, inc=1, device_id={'cp': mate(s)}, device_id_type=MESH)
    for step in (1, n_pl - 1):
        pl.semaphore_signal(barrier, inc=1, device_id={'cpo': lax.rem(z + step, n_pl)}, device_id_type=MESH)
    pl.semaphore_wait(barrier, n_cp + 1)

    def q_copy(j, s):
        dst = gat.at[j, :, pl.ds(s * part, part), :]
        if s == 0:
            return pltpu.make_async_copy(qg.at[c, j], dst, q_r.at[j, 0])
        return remote(qg.at[mate(s), j], dst, q_s.at[s], q_r.at[j, s], cp=mate(s))

    def q_start(j, carry):
        for s in range(n_cp):
            q_copy(j, s).start()
        return carry

    def key_place(who):
        return kv_scr.at[:, pl.ds(pl.multiple_of(who * key_rows, 64), key_rows), :]

    def kv_copy(s):
        if s == 0:
            return pltpu.make_async_copy(kv.at[c], key_place(c), kv_r.at[0])
        return remote(kv.at[mate(s)], key_place(c), kv_s.at[s], kv_r.at[s], cp=mate(s))

    def st_copy(s):
        if s == 0:
            return pltpu.make_async_copy(st.at[c], st_scr.at[0, 0], st_r.at[0])
        return remote(st.at[mate(s)], st_scr.at[0, s], st_s.at[s], st_r.at[s], cp=mate(s))

    lax.fori_loop(0, FIRST, q_start, 0)
    for s in range(n_cp):
        st_copy(s).start()
    for s in range(n_cp):
        kv_copy(s).start()
    lax.fori_loop(FIRST, n_slices, q_start, 0)

    def ups(h):
        return (z < far) & (z >= h - 1)

    def downs(h):
        return (z >= 1) & (z <= n_pl - h)

    def q_hop(j, h, up):
        a, b = (h - 1, h) if up else ((n_pl - h + 1) % n_pl, n_pl - h)
        d = 0 if up else 1
        return remote(gat.at[j, :, slot(a), :], gat.at[j, :, slot(b), :], ag_s.at[d, h - 1], ag_r.at[j, b], cpo=z + 1 if up else z - 1)

    def st_hop(h, up):
        a, b = (h - 1, h) if up else ((n_pl - h + 1) % n_pl, n_pl - h)
        d = 0 if up else 1
        return remote(st_scr.at[a], st_scr.at[b], sz_s.at[d, h - 1], sz_r.at[b], cpo=z + 1 if up else z - 1)

    def send_hop(make, h):
        @pl.when(ups(h))
        def _():
            make(h, True).start()

        @pl.when(downs(h))
        def _():
            make(h, False).start()

    def wait_hop(make, h):
        @pl.when(z >= h)
        def _():
            make(h, True).wait_recv()

        @pl.when(z <= far - h)
        def _():
            make(h, False).wait_recv()

    def ag_first(j):
        for s in range(n_cp):
            copy = q_copy(j, s)
            copy.wait() if s == 0 else copy.wait_recv()
        send_hop(lambda h, up: q_hop(j, h, up), 1)

    def ag_next(j, h):
        wait_hop(lambda h, up: q_hop(j, h, up), h - 1)
        send_hop(lambda h, up: q_hop(j, h, up), h)

    def ag_service(j):
        for h in range(1, n_pl):
            jj = j + AHEAD - (h - 1)

            @pl.when((jj < n_slices) & (jj >= 0))
            def _():
                ag_first(jj) if h == 1 else ag_next(jj, h)

    def rs_copy(j, s, up):
        k = s if up else n_pl - s
        d = 0 if up else 1
        dst = (ru if up else rd).at[j, s - 1]
        return remote(dqp.at[j, slot(k), :], dst, rs_s.at[d, s - 1], rs_r.at[d, j, s - 1], cpo=z + 1 if up else z - 1)

    def rs_step(j, s):
        if s > 1:
            @pl.when((z >= 1) & (z <= s - 1))
            def _():
                rs_copy(j, s - 1, True).wait_recv()
                dqp[j, slot(s), :] += ru[j, s - 2]

            @pl.when((z >= n_pl - s) & (z <= far - 1))
            def _():
                rs_copy(j, s - 1, False).wait_recv()
                dqp[j, slot(n_pl - s), :] += rd[j, s - 2]

        @pl.when(z <= s - 1)
        def _():
            rs_copy(j, s, True).start()

        @pl.when(z >= n_pl - s)
        def _():
            rs_copy(j, s, False).start()

    def dq_copy(j, s):
        src = dqb.at[j, pl.ds(s * part, part), :]
        if s == 0:
            return pltpu.make_async_copy(src, dq_out.at[c, j], dq_r.at[0])
        return remote(src, dq_out.at[c, j], dq_s.at[s], dq_r.at[s], cp=mate(s))

    def rs_final(j):
        @pl.when(z >= 1)
        def _():
            rs_copy(j, far, True).wait_recv()
            dqp[j, slot(0), :] += ru[j, far - 1]

        @pl.when(z <= far - 1)
        def _():
            rs_copy(j, far, False).wait_recv()
            dqp[j, slot(0), :] += rd[j, far - 1]

        dqb[j] = (dqp[j, slot(0), :] * scale).astype(jnp.bfloat16)
        for s in range(n_cp):
            dq_copy(j, s).start()

    def rs_service(j):
        for s in range(1, n_pl + 1):
            jj = j - s

            @pl.when((jj >= 0) & (jj < n_slices))
            def _():
                rs_step(jj, s) if s < n_pl else rs_final(jj)

    def compute(j):
        cols16 = [st_scr[k, s, pl.ds(2 * j, 2), :] for k in range(n_pl) for s in range(n_cp)]
        stat_t = jnp.concatenate(cols16, axis=0).T
        for i in range(n_pl * n_cp):
            rr = pl.ds(i * part, part)
            l_scr[rr, :] = jnp.broadcast_to(stat_t[:part, 2 * i:2 * i + 1] * LOG2E, (part, 128))
            d_scr[rr, :] = jnp.broadcast_to(stat_t[:part, 2 * i + 1:2 * i + 2], (part, 128))
        qt_scr[...] = gat[j, 0].T
        gt_scr[...] = gat[j, 1].T

        def scores(r, kt, vt):
            rr = pl.ds(r * SUB, SUB)
            s = jnp.dot(gat[j, 0, rr, :], kt, preferred_element_type=jnp.float32)
            dp = jnp.dot(gat[j, 1, rr, :], vt, preferred_element_type=jnp.float32)
            return s, dp

        def probs(r, s, dp, masked):
            rr = pl.ds(r * SUB, SUB)
            lb = l_scr[rr, :]
            db = d_scr[rr, :]
            lb = jnp.concatenate([lb, lb], axis=1)
            db = jnp.concatenate([db, db], axis=1)
            p = jnp.exp2(s * (scale * LOG2E) - lb)
            if masked:
                pos = qpos[rr, :]
                pos = jnp.concatenate([pos, pos], axis=1)
                key = lax.broadcasted_iota(jnp.int32, (SUB, KEY_BLOCK), 1)
                p = jnp.where(key <= pos, p, 0.0)
            return p.astype(jnp.bfloat16), (p * (dp - db)).astype(jnp.bfloat16)

        def block(b, masked):
            cols = pl.ds(pl.multiple_of(b * KEY_BLOCK, KEY_BLOCK), KEY_BLOCK)
            kt = kt_scr[:, cols]
            vt = vt_scr[:, cols]
            kk = kv_scr[0, cols, :]
            acc_v = acc_k = held = None
            n_sub = rows // SUB
            for r in range(n_sub + 1):
                if r < n_sub:
                    s, dp = scores(r, kt, vt)
                if held is not None:
                    q = pl.ds((r - 1) * SUB, SUB)
                    p, ds = held
                    av = jnp.dot(gt_scr[:, q], p, preferred_element_type=jnp.float32)
                    ak = jnp.dot(qt_scr[:, q], ds, preferred_element_type=jnp.float32)
                    acc_v = av if acc_v is None else acc_v + av
                    acc_k = ak if acc_k is None else acc_k + ak
                    dq = jnp.dot(ds, kk, preferred_element_type=jnp.float32)
                    if masked:
                        dqp[j, q, :] = dq
                    else:
                        dqp[j, q, :] += dq
                if r < n_sub:
                    held = probs(r, s, dp, masked)
            dv_scr[:, cols] += acc_v
            dk_scr[:, cols] += acc_k

        first_block = lax.div(z, far) * (n_pref_last + j - (n_blocks - 1)) + n_blocks - 1
        block(first_block, True)

        def step(b, carry):
            block(b, False)
            return carry

        lax.fori_loop(0, first_block, step, 0)

    dk_scr[...] = jnp.zeros_like(dk_scr)
    dv_scr[...] = jnp.zeros_like(dv_scr)
    for j in range(FIRST):
        ag_first(j)
    for s in range(n_cp):
        copy = st_copy(s)
        copy.wait() if s == 0 else copy.wait_recv()
    send_hop(st_hop, 1)
    for h in range(2, n_pl):
        for j in range(FIRST):
            ag_next(j, h)
        wait_hop(st_hop, h - 1)
        send_hop(st_hop, h)
    for s in range(n_cp):
        copy = kv_copy(s)
        copy.wait() if s == 0 else copy.wait_recv()

    def turn(b, carry):
        cols = pl.ds(pl.multiple_of(b * KEY_BLOCK, KEY_BLOCK), KEY_BLOCK)
        kt_scr[:, cols] = kv_scr[0, cols, :].T
        vt_scr[:, cols] = kv_scr[1, cols, :].T
        return carry

    lax.fori_loop(0, n_blocks, turn, 0)
    wait_hop(st_hop, far)

    for h in range(1, n_pl):
        for j in range(FIRST, AHEAD - (h - 1)):
            if j < n_slices:
                ag_first(j) if h == 1 else ag_next(j, h)

    def slice_step(j, carry):
        ag_service(j)
        rs_service(j)
        wait_hop(lambda h, up: q_hop(j, h, up), far)
        compute(j)
        return carry

    lax.fori_loop(0, n_slices, slice_step, 0)
    rs_service(n_slices)

    def home(src, out, s, n):
        place = src.at[pl.ds(pl.multiple_of((mate(s)) * key_rows, 64), key_rows), :]
        if s == 0:
            return pltpu.make_async_copy(place, out.at[c], dk_r.at[n, 0])
        return remote(place, out.at[c], dk_s.at[n, s], dk_r.at[n, s], cp=mate(s))

    def turn_back(acc, out, factor):
        def go(b, carry):
            cols = pl.ds(pl.multiple_of(b * KEY_BLOCK, KEY_BLOCK), KEY_BLOCK)
            out[cols, :] = acc[:, cols].T * factor
            return carry

        lax.fori_loop(0, n_blocks, go, 0)

    pairs = ((dv_scr, dvo, dv_out, 1.0), (dk_scr, dko, dk_out, scale))
    for n, (acc, held, out, factor) in enumerate(pairs):
        turn_back(acc, held, factor)
        for s in range(n_cp):
            home(held, out, (s + 1) % n_cp, n).start()

    def flush(j, carry):
        rs_service(j)
        return carry

    lax.fori_loop(n_slices + 1, n_slices + n_pl, flush, 0)

    for s in range(n_cp):
        whole = dqb.at[:, pl.ds(s * part, part), :]
        if s == 0:
            pltpu.make_async_copy(whole, dq_out.at[c], dq_r.at[0]).wait()
        else:
            remote(whole, dq_out.at[mate(s)], dq_s.at[s], dq_r.at[s], cp=mate(s)).wait()
            remote(qg.at[mate(s)], gat.at[:, :, pl.ds(s * part, part), :], q_s.at[s], q_r.at[0, s], cp=mate(s)).wait_send()
            kv_copy(s).wait_send()
            st_copy(s).wait_send()
        for n, (acc, held, out, factor) in enumerate(pairs):
            home(held, out, s, n).wait()
    for h in range(1, n_pl):
        for up in (True, False):
            cond = ups(h) if up else downs(h)

            @pl.when(cond)
            def _():
                d = 0 if up else 1
                whole = gat.at[:, :, slot(0), :]
                remote(whole, whole, ag_s.at[d, h - 1], ag_r.at[0, 1], cpo=z + 1 if up else z - 1).wait_send()
                st_hop(h, up).wait_send()

            cond = (z <= h - 1) if up else (z >= n_pl - h)

            @pl.when(cond)
            def _():
                d = 0 if up else 1
                whole = dqp.at[:, slot(0), :]
                remote(whole, whole, rs_s.at[d, h - 1], rs_r.at[d, 0, 0], cpo=z + 1 if up else z - 1).wait_send()


def solution(mesh):
    n_cpo = mesh.shape['cpo']
    n_cp = mesh.shape['cp']
    row_spec = P(None, CP_AXES, 'heads', None)
    stat_spec = P(None, CP_AXES, 'heads')
    key_spec = P(CP_AXES, 'heads', None)

    def local_grads(queries, attn_out, grad_out, log_sum_exp, key_cache, value_cache):
        n_slices, rows_dev, q_heads, head_dim = queries.shape
        key_rows, kv_heads, _ = key_cache.shape
        group = q_heads // kv_heads
        slice_len = rows_dev * n_cp * n_cpo
        plane_keys = key_rows * n_cp
        prefix = plane_keys * n_cpo - n_slices * slice_len
        n_pref_last = (prefix - plane_keys * (n_cpo - 1)) // KEY_BLOCK
        scale = head_dim ** -0.5
        part = rows_dev * group
        piece = n_cp * part
        rows = n_cpo * piece
        bf, f32 = jnp.bfloat16, jnp.float32
        z = lax.axis_index('cpo')
        c = lax.axis_index('cp')

        delta = jnp.sum(grad_out.astype(f32) * attn_out.astype(f32), axis=-1)
        st = jnp.stack([log_sum_exp, delta], axis=1).reshape(n_slices, 2, rows_dev, kv_heads, group)
        st = st.transpose(3, 0, 1, 2, 4).reshape(kv_heads, n_slices * 2, part)
        st = jnp.pad(st, ((0, 0), (0, -(n_slices * 2) % 8), (0, 128 - part)))
        qg = jnp.stack([queries, grad_out], axis=1).reshape(n_slices, 2, rows_dev, kv_heads, group, head_dim)
        qg = jnp.transpose(qg, (3, 0, 1, 2, 4, 5)).reshape(kv_heads, n_slices, 2, part, head_dim)
        kv = jnp.transpose(jnp.stack([key_cache, value_cache]), (2, 0, 1, 3))

        r = jnp.arange(rows)
        plane = (z - r // piece) % n_cpo
        tok = plane * n_cp * rows_dev + (c ^ ((r % piece) // part)) * rows_dev + (r % part) // group
        tok = jnp.where(z == n_cpo - 1, tok, slice_len)
        qpos = jnp.broadcast_to(tok[:, None], (rows, 128)).astype(jnp.int32)

        any_spec = pl.BlockSpec(memory_space=pl.ANY)
        vmem = pl.BlockSpec(memory_space=pltpu.VMEM)
        dma = pltpu.SemaphoreType.DMA
        dq, dk, dv = pl.pallas_call(
            functools.partial(attention_kernel, n_cpo, n_cp, n_pref_last, scale),
            out_shape=[
                jax.ShapeDtypeStruct((kv_heads, n_slices, part, head_dim), bf),
                jax.ShapeDtypeStruct((kv_heads, key_rows, head_dim), f32),
                jax.ShapeDtypeStruct((kv_heads, key_rows, head_dim), f32),
            ],
            in_specs=[any_spec] * 3 + [vmem],
            out_specs=[any_spec] * 3,
            scratch_shapes=[
                pltpu.VMEM((n_slices, 2, rows, head_dim), bf),
                pltpu.VMEM((2, plane_keys, head_dim), bf),
                pltpu.VMEM((head_dim, plane_keys), bf),
                pltpu.VMEM((head_dim, plane_keys), bf),
                pltpu.VMEM((n_cpo, n_cp) + st.shape[1:], f32),
                pltpu.VMEM((n_slices, rows, head_dim), f32),
                pltpu.VMEM((n_slices, n_cpo - 1, piece, head_dim), f32),
                pltpu.VMEM((n_slices, n_cpo - 1, piece, head_dim), f32),
                pltpu.VMEM((n_slices, piece, head_dim), bf),
                pltpu.VMEM((head_dim, plane_keys), f32),
                pltpu.VMEM((head_dim, plane_keys), f32),
                pltpu.VMEM((plane_keys, head_dim), f32),
                pltpu.VMEM((plane_keys, head_dim), f32),
                pltpu.VMEM((head_dim, rows), bf),
                pltpu.VMEM((head_dim, rows), bf),
                pltpu.VMEM((rows, 128), f32),
                pltpu.VMEM((rows, 128), f32),
                dma((n_cp,)), dma((n_slices, n_cp)),
                dma((n_cp,)), dma((n_cp,)),
                dma((n_cp,)), dma((n_cp,)),
                dma((2, n_cpo - 1)), dma((n_cpo,)),
                dma((2, n_cpo - 1)), dma((n_slices, n_cpo)),
                dma((2, n_cpo - 1)), dma((2, n_slices, n_cpo - 1)),
                dma((n_cp,)), dma((n_cp,)),
                dma((2, n_cp)), dma((2, n_cp)),
            ],
            compiler_params=pltpu.CompilerParams(vmem_limit_bytes=63 * 1024 * 1024, collective_id=0, has_side_effects=True),
            name='attention_backward',
        )(qg, kv, st, qpos)

        dq = dq.reshape(kv_heads, n_slices, rows_dev, group, head_dim)
        grad_query = jnp.transpose(dq, (1, 2, 0, 3, 4)).reshape(queries.shape)
        return grad_query, jnp.transpose(dk, (1, 0, 2)), jnp.transpose(dv, (1, 0, 2))

    return jax.shard_map(local_grads, mesh=mesh, in_specs=(row_spec, row_spec, row_spec, stat_spec, key_spec, key_spec), out_specs=(row_spec, key_spec, key_spec), check_vma=False)
```

time: 1840 us -> 359 us (0.20)
  waiting for transfers between devices: 806 us -> 0 us
  matrix products: 656 us -> 0 us
  Pallas kernels: 0 us -> 325 us
  blocking collectives: 233 us -> 0 us
  local copies, waits for them, and re-layouts: 73.9 us -> 24.5 us
  other arithmetic: 42.3 us -> 7.87 us
    reduce_scatter x12 -> x0, waiting for transfers between devices: 770 us -> none  [local_grads(): lax.psum_scatter(dq_part, CP_AXES, scatter_dimension=0, tiled=True)]
    dot_general x120 -> x0, matrix products: 656 us -> none  [the longest x24 191 us: block_step(): jnp.einsum('rhgd,khd->hrgk', g_blk, value_part, preferred_element_type=jn...]
    pallas_call x0 -> x1, Pallas kernels: none -> 325 us  [local_grads(): pl.pallas_call(functools.partial(attention_kernel, n_cpo, n_cp, n_pref_la...]
    all_gather x12 -> x0, blocking collectives: 233 us -> none  [local_grads(): stat_all = lax.all_gather(row_stats[slice_idx], CP_AXES, axis=0, tiled=True)]
    add x60 -> x0, other arithmetic: 21.6 us -> none  [the longest x24 15.5 us: block_step(): q_pos = row_start + jnp.arange(q_blk.shape[0])]
    unnamed x36 -> x0, waiting for transfers between devices: 20 us -> none
  transfers between devices with their start and end apart: 36 -> 0, of which waited for: 13 -> 0; matrix products, arithmetic and copies ran while one was open for 38% -> 0% of each run, Pallas kernels for 0% -> 0%
where the time goes in v1:
time: 359 us; the launch traced here: 358 us
  Pallas kernels  325 us (91%)
  local copies, waits for them, and re-layouts  24.5 us (7%)
  other arithmetic  7.87 us (2%)
    pallas_call x1, Pallas kernels, local_grads(): pl.pallas_call(functools.partial(attention_kernel, n_cpo, n_cp, n_pref_la...  325 us
    unnamed x17, local copies, waits for them, and re-layouts  13.3 us

profile of v1, /device:TPU:0, one launch (start us, length us, event | category | flops | bytes accessed | tf_op | source)
XLA Modules:
  0.0 357.9 jit_solution(4498265397937691380)
XLA Ops:
  0.6 0.0 copy-start.6
  0.7 2.1 multiply_reduce_fusion
  2.8 0.0 copy-start.5
  2.8 0.0 copy-done.6
  2.8 0.2 copy.42
  3.1 0.6 copy.44
  3.7 0.4 reshape.87
  4.1 0.0 copy-start
  4.1 0.6 pad.4.refs_2_
  4.7 1.1 broadcast_in_dim.11.refs_3_
  5.8 0.0 copy-done.5
  5.8 1.7 copy.38
  7.4 0.0 copy-done
  7.5 1.7 copy.39
  9.1 4.1 %pad_maximum_fusion = bf16[12,2,16,4,5,128]{5,1,4,2,0,3:T(2,128)(2,1)S(1)} fusion(bf16[12,1,16,4,5,128]{5,1,4,2,0,3:T(2,128)(2,1)S(1)} %copy.39, bf16[12,1,16,4,5,128]{5,1,4,2,0,3:T(2,128)(2,1)S(1)} %copy.38), kind=kLoop, calls=%fused_computation.1 | loop fusion | flops 3932160 | bytes 3932160 | tf_op jit(solution)/shard_map/stack | solution.py:378
  13.2 0.0 copy-start.3
  13.2 0.0 copy-start.4
  13.2 1.6 copy.45.refs_0_
  14.8 0.0 copy-done.3
  14.8 0.8 copy-done.4
  15.6 0.3 copy_bitcast_fusion
  15.9 1.7 maximum_bitcast_fusion.refs_1_
  17.6 324.8 %attention_backward.1 = (bf16[4,12,80,128]{3,2,1,0:T(8,128)(2,1)}, f32[4,1216,128]{2,1,0:T(8,128)}, f32[4,1216,128]{2,1,0:T(8,128)}) custom-call(bf16[4,12,2,80,128]{4,3,2,1,0:T(8,128)(2,1)} %copy.45.refs_0_, bf16[4,2,1216,128]{3,2,1,0:T(8,128)(2,1)} %maximum_bitcast_fusion.refs_1_, f32[4,24,128]{2,1,0:T(8,128)} %pad.4.refs_2_, ...), custom_call_target="tpu_custom_call" | custom-call | tf_op jit(solution)/shard_map/attention_backward/pallas_call | solution.py:391
  342.4 0.0 copy-start.2
  342.4 2.1 copy.46
  344.5 1.1 copy.47
  345.6 0.0 copy-done.2
  345.6 0.0 copy-start.1
  345.6 6.2 %copy.48 = f32[1216,4,128]{2,1,0:T(4,128)} copy(f32[1216,4,128]{2,0,1:T(8,128)S(1)} %bitcast.27) | data formatting | bytes 4980736
  351.8 0.0 copy-done.1
  351.8 6.2 %copy.49 = f32[1216,4,128]{2,1,0:T(4,128)} copy(f32[1216,4,128]{2,0,1:T(8,128)S(1)} %bitcast.26) | data formatting | bytes 4980736
  (3 shorter events, 0.1 us)
Async XLA Ops:
  0.6 2.2 copy-start.6
  2.8 3.0 copy-start.5
  4.1 3.4 copy-start
  13.2 1.6 copy-start.3
  13.2 2.4 copy-start.4
  342.4 3.2 copy-start.2
  345.6 6.2 %copy-start.1 = (f32[4,1216,128]{2,1,0:T(8,128)S(1)}, f32[4,1216,128]{2,1,0:T(8,128)}, u32[]{:S(2)}) copy-start(f32[4,1216,128]{2,1,0:T(8,128)} %get-tuple-element.8) | copy-start | bytes 7471108

commit v2 on v1

--- a/solution.py
+++ b/solution.py
@@ -121,11 +121,11 @@
         wait_hop(lambda h, up: q_hop(j, h, up), h - 1)
         send_hop(lambda h, up: q_hop(j, h, up), h)
 
-    def ag_service(j):
+    def ag_service(t, due):
         for h in range(1, n_pl):
-            jj = j + AHEAD - (h - 1)
-
-            @pl.when((jj < n_slices) & (jj >= 0))
+            jj = t + AHEAD - (h - 1)
+
+            @pl.when(due & (jj < n_slices))
             def _():
                 ag_first(jj) if h == 1 else ag_next(jj, h)
 
@@ -176,15 +176,19 @@
         for s in range(n_cp):
             dq_copy(j, s).start()
 
-    def rs_service(j):
+    def rs_service(u, due, low, high):
         for s in range(1, n_pl + 1):
-            jj = j - s
-
-            @pl.when((jj >= 0) & (jj < n_slices))
+            jj = u - s
+
+            @pl.when(due & (jj >= low) & (jj < high))
             def _():
                 rs_step(jj, s) if s < n_pl else rs_final(jj)
 
-    def compute(j):
+    def compute(j, low, high, fresh):
+        @pl.when(fresh)
+        def _():
+            dqp[j] = jnp.zeros(dqp.shape[1:], jnp.float32)
+
         cols16 = [st_scr[k, s, pl.ds(2 * j, 2), :] for k in range(n_pl) for s in range(n_cp)]
         stat_t = jnp.concatenate(cols16, axis=0).T
         for i in range(n_pl * n_cp):
@@ -232,23 +236,23 @@
                     acc_v = av if acc_v is None else acc_v + av
                     acc_k = ak if acc_k is None else acc_k + ak
                     dq = jnp.dot(ds, kk, preferred_element_type=jnp.float32)
-                    if masked:
-                        dqp[j, q, :] = dq
-                    else:
-                        dqp[j, q, :] += dq
+                    dqp[j, q, :] += dq
                 if r < n_sub:
                     held = probs(r, s, dp, masked)
             dv_scr[:, cols] += acc_v
             dk_scr[:, cols] += acc_k
 
-        first_block = lax.div(z, far) * (n_pref_last + j - (n_blocks - 1)) + n_blocks - 1
-        block(first_block, True)
+        edge = lax.div(z, far) * (n_pref_last + j - (n_blocks - 1)) + n_blocks - 1
 
         def step(b, carry):
             block(b, False)
             return carry
 
-        lax.fori_loop(0, first_block, step, 0)
+        lax.fori_loop(low, lax.min(high, edge), step, 0)
+
+        @pl.when((edge >= low) & (edge < high))
+        def _():
+            block(edge, True)
 
     dk_scr[...] = jnp.zeros_like(dk_scr)
     dv_scr[...] = jnp.zeros_like(dv_scr)
@@ -263,9 +267,9 @@
             ag_next(j, h)
         wait_hop(st_hop, h - 1)
         send_hop(st_hop, h)
-    for s in range(n_cp):
-        copy = kv_copy(s)
-        copy.wait() if s == 0 else copy.wait_recv()
+    y = lax.div(c, 2)
+    own = (y * ((n_blocks + 1) // 2), n_blocks // 2 + y * (n_blocks - n_blocks // 2))
+    other = ((1 - y) * (n_blocks // 2), n_blocks - y * (n_blocks // 2))
 
     def turn(b, carry):
         cols = pl.ds(pl.multiple_of(b * KEY_BLOCK, KEY_BLOCK), KEY_BLOCK)
@@ -273,46 +277,78 @@
         vt_scr[:, cols] = kv_scr[1, cols, :].T
         return carry
 
-    lax.fori_loop(0, n_blocks, turn, 0)
+    kv_copy(0).wait()
+    kv_copy(1).wait_recv()
+    lax.fori_loop(own[0], own[1], turn, 0)
     wait_hop(st_hop, far)
 
-    for h in range(1, n_pl):
-        for j in range(FIRST, AHEAD - (h - 1)):
-            if j < n_slices:
-                ag_first(j) if h == 1 else ag_next(j, h)
-
-    def slice_step(j, carry):
-        ag_service(j)
-        rs_service(j)
-        wait_hop(lambda h, up: q_hop(j, h, up), far)
-        compute(j)
-        return carry
-
-    lax.fori_loop(0, n_slices, slice_step, 0)
-    rs_service(n_slices)
-
     def home(src, out, s, n):
-        place = src.at[pl.ds(pl.multiple_of((mate(s)) * key_rows, 64), key_rows), :]
+        place = src.at[pl.ds(pl.multiple_of(mate(s) * key_rows, 64), key_rows), :]
         if s == 0:
             return pltpu.make_async_copy(place, out.at[c], dk_r.at[n, 0])
         return remote(place, out.at[c], dk_s.at[n, s], dk_r.at[n, s], cp=mate(s))
 
-    def turn_back(acc, out, factor):
-        def go(b, carry):
-            cols = pl.ds(pl.multiple_of(b * KEY_BLOCK, KEY_BLOCK), KEY_BLOCK)
-            out[cols, :] = acc[:, cols].T * factor
-            return carry
-
-        lax.fori_loop(0, n_blocks, go, 0)
-
     pairs = ((dv_scr, dvo, dv_out, 1.0), (dk_scr, dko, dk_out, scale))
-    for n, (acc, held, out, factor) in enumerate(pairs):
-        turn_back(acc, held, factor)
-        for s in range(n_cp):
-            home(held, out, (s + 1) % n_cp, n).start()
-
-    def flush(j, carry):
-        rs_service(j)
+
+    def go_home(span, mates):
+        for n, (acc, held, out, factor) in enumerate(pairs):
+            def turn_back(b, carry):
+                cols = pl.ds(pl.multiple_of(b * KEY_BLOCK, KEY_BLOCK), KEY_BLOCK)
+                held[cols, :] = acc[:, cols].T * factor
+                return carry
+
+            lax.fori_loop(span[0], span[1], turn_back, 0)
+            for s in mates:
+                home(held, out, s, n).start()
+
+    half = n_slices // 2
+
+    def item(i, carry):
+        early = i < 2 * half
+        late = i >= half + n_slices
+        j = jnp.where(i < 2, i, jnp.where(i < 4, i - 2, jnp.where(early, lax.div(i, 2), jnp.where(late, i - n_slices, i - half))))
+        is_own = jnp.where(i < 2, 1, jnp.where(i < 4, 0, jnp.where(early, 1 - lax.rem(i, 2), jnp.where(late, 1, 0))))
+        is_first = jnp.where(i < 2, 1, jnp.where(i < 4, 0, jnp.where(early, 1 - lax.rem(i, 2), jnp.where(late, 0, 1))))
+        low = is_own * own[0] + (1 - is_own) * other[0]
+        high = is_own * own[1] + (1 - is_own) * other[1]
+        even = lax.rem(i, 2) == 0
+
+        for h in range(1, n_pl):
+            for jj in range(FIRST, min(AHEAD - (h - 1), n_slices)):
+                @pl.when(i == 1)
+                def _():
+                    ag_first(jj) if h == 1 else ag_next(jj, h)
+
+        ag_service(jnp.where(i < 8, lax.div(i, 2) - 1, i - 5), ((i >= 2) & even) | (i > 8))
+
+        @pl.when(i == 2)
+        def _():
+            for s in range(2, n_cp):
+                kv_copy(s).wait_recv()
+            lax.fori_loop(other[0], other[1], turn, 0)
+
+        rs_service(
+            jnp.where(i <= 2 * half, lax.div(i, 2), i - half),
+            (i == 3) | ((i >= 4) & (i <= 2 * half) & even) | ((i > 2 * half) & (i < 2 * half + n_pl)), 0, half)
+        rs_service(i - n_slices, i > half + n_slices, half, n_slices)
+
+        @pl.when(i == half + n_slices)
+        def _():
+            go_home(other, (2, 3))
+
+        @pl.when(is_first == 1)
+        def _():
+            wait_hop(lambda h, up: q_hop(j, h, up), far)
+
+        compute(j, low, high, is_first == 1)
+        return carry
+
+    lax.fori_loop(0, 2 * n_slices, item, 0)
+    rs_service(n_slices, z >= 0, half, n_slices)
+    go_home(own, (1, 0))
+
+    def flush(u, carry):
+        rs_service(u, u >= 0, half, n_slices)
         return carry
 
     lax.fori_loop(n_slices + 1, n_slices + n_pl, flush, 0)

time: 359 us -> 354 us (0.986)
  Pallas kernels: 325 us -> 320 us
    pallas_call x1, Pallas kernels: 325 us -> 320 us  [local_grads(): pl.pallas_call(functools.partial(attention_kernel, n_cpo, n_cp, n_pref_la...]
where the time goes in v2:
time: 354 us
  Pallas kernels  320 us (90%)
  local copies, waits for them, and re-layouts  24.5 us (7%)
  other arithmetic  7.87 us (2%)
    pallas_call x1, Pallas kernels, local_grads(): pl.pallas_call(functools.partial(attention_kernel, n_cpo, n_cp, n_pref_la...  320 us
    unnamed x17, local copies, waits for them, and re-layouts  13.3 us

profile of v2, /device:TPU:0, one launch (start us, length us, event | category | flops | bytes accessed | tf_op | source)
XLA Modules:
  0.0 353.6 jit_solution(8682518538164441987)
XLA Ops:
  0.6 0.0 copy-start.6
  0.7 2.1 multiply_reduce_fusion
  2.8 0.0 copy-start.5
  2.8 0.0 copy-done.6
  2.8 0.2 copy.42
  3.1 0.6 copy.44
  3.7 0.4 reshape.87
  4.1 0.0 copy-start
  4.1 0.6 pad.4.refs_2_
  4.7 1.1 broadcast_in_dim.11.refs_3_
  5.8 0.0 copy-done.5
  5.8 1.7 copy.38
  7.4 0.0 copy-done
  7.5 1.7 copy.39
  9.1 4.1 %pad_maximum_fusion = bf16[12,2,16,4,5,128]{5,1,4,2,0,3:T(2,128)(2,1)S(1)} fusion(bf16[12,1,16,4,5,128]{5,1,4,2,0,3:T(2,128)(2,1)S(1)} %copy.39, bf16[12,1,16,4,5,128]{5,1,4,2,0,3:T(2,128)(2,1)S(1)} %copy.38), kind=kLoop, calls=%fused_computation.1 | loop fusion | flops 3932160 | bytes 3932160 | tf_op jit(solution)/shard_map/stack | solution.py:414
  13.2 0.0 copy-start.3
  13.2 0.0 copy-start.4
  13.2 1.6 copy.45.refs_0_
  14.8 0.0 copy-done.3
  14.8 0.8 copy-done.4
  15.6 0.3 copy_bitcast_fusion
  15.9 1.7 maximum_bitcast_fusion.refs_1_
  17.6 320.4 %attention_backward.1 = (bf16[4,12,80,128]{3,2,1,0:T(8,128)(2,1)}, f32[4,1216,128]{2,1,0:T(8,128)}, f32[4,1216,128]{2,1,0:T(8,128)}) custom-call(bf16[4,12,2,80,128]{4,3,2,1,0:T(8,128)(2,1)} %copy.45.refs_0_, bf16[4,2,1216,128]{3,2,1,0:T(8,128)(2,1)} %maximum_bitcast_fusion.refs_1_, f32[4,24,128]{2,1,0:T(8,128)} %pad.4.refs_2_, ...), custom_call_target="tpu_custom_call" | custom-call | tf_op jit(solution)/shard_map/attention_backward/pallas_call | solution.py:427
  338.0 0.0 copy-start.2
  338.0 2.1 copy.46
  340.1 1.1 copy.47
  341.2 0.0 copy-done.2
  341.2 0.0 copy-start.1
  341.2 6.2 %copy.48 = f32[1216,4,128]{2,1,0:T(4,128)} copy(f32[1216,4,128]{2,0,1:T(8,128)S(1)} %bitcast.27) | data formatting | bytes 4980736
  347.4 0.0 copy-done.1
  347.4 6.2 %copy.49 = f32[1216,4,128]{2,1,0:T(4,128)} copy(f32[1216,4,128]{2,0,1:T(8,128)S(1)} %bitcast.26) | data formatting | bytes 4980736
  (3 shorter events, 0.1 us)
Async XLA Ops:
  0.6 2.2 copy-start.6
  2.8 3.0 copy-start.5
  4.1 3.4 copy-start
  13.2 1.6 copy-start.3
  13.2 2.4 copy-start.4
  338.0 3.2 copy-start.2
  341.2 6.2 %copy-start.1 = (f32[4,1216,128]{2,1,0:T(8,128)S(1)}, f32[4,1216,128]{2,1,0:T(8,128)}, u32[]{:S(2)}) copy-start(f32[4,1216,128]{2,1,0:T(8,128)} %get-tuple-element.8) | copy-start | bytes 7471108

commit v3 on v2

--- a/solution.py
+++ b/solution.py
@@ -13,18 +13,19 @@
 KEY_BLOCK = 256
 SUB = 256
 AHEAD = 4
+TOGETHER = 3
 FIRST = 2
 
 
 def attention_kernel(n_pl, n_cp, n_pref_last, scale, *refs):
-    (qg, kv, st, qpos, dq_out, dk_out, dv_out) = refs[:7]
-    (gat, kv_scr, kt_scr, vt_scr, st_scr, dqp, ru, rd, dqb, dk_scr, dv_scr, dko, dvo, qt_scr, gt_scr, l_scr, d_scr) = refs[7:24]
-    (q_s, q_r, kv_s, kv_r, st_s, st_r, sz_s, sz_r, ag_s, ag_r, rs_s, rs_r, dq_s, dq_r, dk_s, dk_r) = refs[24:]
+    (q_in, g_in, k_in, v_in, st, qpos, dq_out, dk_out, dv_out) = refs[:9]
+    (gat, kv_scr, kt_scr, vt_scr, st_scr, dqp, ru, rd, dqb, dk_scr, dv_scr, dko, dvo, turned, l_scr, d_scr) = refs[9:25]
+    (q_s, q_r, kv_s, kv_r, st_s, st_r, sz_s, sz_r, ag_s, ag_r, rs_s, rs_r, dq_s, dq_r, dk_s, dk_r) = refs[25:]
     n_slices = gat.shape[0]
     rows = gat.shape[2]
     piece = rows // n_pl
     part = piece // n_cp
-    key_rows = kv.shape[2]
+    key_rows = k_in.shape[1]
     n_blocks = kv_scr.shape[1] // KEY_BLOCK
     far = n_pl - 1
     z = lax.axis_index('cpo')
@@ -46,24 +47,31 @@
         pl.semaphore_signal(barrier, inc=1, device_id={'cpo': lax.rem(z + step, n_pl)}, device_id_type=MESH)
     pl.semaphore_wait(barrier, n_cp + 1)
 
-    def q_copy(j, s):
-        dst = gat.at[j, :, pl.ds(s * part, part), :]
-        if s == 0:
-            return pltpu.make_async_copy(qg.at[c, j], dst, q_r.at[j, 0])
-        return remote(qg.at[mate(s), j], dst, q_s.at[s], q_r.at[j, s], cp=mate(s))
+    def q_copies(j, s):
+        out = []
+        for t, src in enumerate((q_in, g_in)):
+            dst = gat.at[j, t, pl.ds(s * part, part), :]
+            if s == 0:
+                out.append(pltpu.make_async_copy(src.at[j, c], dst, q_r.at[j, 0, t]))
+            else:
+                out.append(remote(src.at[j, mate(s)], dst, q_s.at[s, t], q_r.at[j, s, t], cp=mate(s)))
+        return out
 
     def q_start(j, carry):
         for s in range(n_cp):
-            q_copy(j, s).start()
+            for copy in q_copies(j, s):
+                copy.start()
         return carry
 
-    def key_place(who):
-        return kv_scr.at[:, pl.ds(pl.multiple_of(who * key_rows, 64), key_rows), :]
-
-    def kv_copy(s):
-        if s == 0:
-            return pltpu.make_async_copy(kv.at[c], key_place(c), kv_r.at[0])
-        return remote(kv.at[mate(s)], key_place(c), kv_s.at[s], kv_r.at[s], cp=mate(s))
+    def kv_copies(s):
+        out = []
+        for t, src in enumerate((k_in, v_in)):
+            dst = kv_scr.at[t, pl.ds(pl.multiple_of(c * key_rows, 64), key_rows), :]
+            if s == 0:
+                out.append(pltpu.make_async_copy(src.at[c], dst, kv_r.at[0, t]))
+            else:
+                out.append(remote(src.at[mate(s)], dst, kv_s.at[s, t], kv_r.at[s, t], cp=mate(s)))
+        return out
 
     def st_copy(s):
         if s == 0:
@@ -74,7 +82,8 @@
     for s in range(n_cp):
         st_copy(s).start()
     for s in range(n_cp):
-        kv_copy(s).start()
+        for copy in kv_copies(s):
+            copy.start()
     lax.fori_loop(FIRST, n_slices, q_start, 0)
 
     def ups(h):
@@ -113,8 +122,8 @@
 
     def ag_first(j):
         for s in range(n_cp):
-            copy = q_copy(j, s)
-            copy.wait() if s == 0 else copy.wait_recv()
+            for copy in q_copies(j, s):
+                copy.wait() if s == 0 else copy.wait_recv()
         send_hop(lambda h, up: q_hop(j, h, up), 1)
 
     def ag_next(j, h):
@@ -158,8 +167,8 @@
     def dq_copy(j, s):
         src = dqb.at[j, pl.ds(s * part, part), :]
         if s == 0:
-            return pltpu.make_async_copy(src, dq_out.at[c, j], dq_r.at[0])
-        return remote(src, dq_out.at[c, j], dq_s.at[s], dq_r.at[s], cp=mate(s))
+            return pltpu.make_async_copy(src, dq_out.at[j, c], dq_r.at[0])
+        return remote(src, dq_out.at[j, c], dq_s.at[s], dq_r.at[s], cp=mate(s))
 
     def rs_final(j):
         @pl.when(z >= 1)
@@ -195,8 +204,12 @@
             rr = pl.ds(i * part, part)
             l_scr[rr, :] = jnp.broadcast_to(stat_t[:part, 2 * i:2 * i + 1] * LOG2E, (part, 128))
             d_scr[rr, :] = jnp.broadcast_to(stat_t[:part, 2 * i + 1:2 * i + 2], (part, 128))
-        qt_scr[...] = gat[j, 0].T
-        gt_scr[...] = gat[j, 1].T
+
+        @pl.when(fresh)
+        def _():
+            turned[j, 0] = gat[j, 0].T
+            turned[j, 1] = gat[j, 1].T
+
 
         def scores(r, kt, vt):
             rr = pl.ds(r * SUB, SUB)
@@ -218,41 +231,51 @@
                 p = jnp.where(key <= pos, p, 0.0)
             return p.astype(jnp.bfloat16), (p * (dp - db)).astype(jnp.bfloat16)
 
-        def block(b, masked):
-            cols = pl.ds(pl.multiple_of(b * KEY_BLOCK, KEY_BLOCK), KEY_BLOCK)
-            kt = kt_scr[:, cols]
-            vt = vt_scr[:, cols]
-            kk = kv_scr[0, cols, :]
-            acc_v = acc_k = held = None
+        def blocks(first, count, masked=False):
+            cols = [pl.ds(pl.multiple_of((first + n) * KEY_BLOCK, KEY_BLOCK), KEY_BLOCK) for n in range(count)]
             n_sub = rows // SUB
-            for r in range(n_sub + 1):
-                if r < n_sub:
-                    s, dp = scores(r, kt, vt)
+            held = None
+            for i in range(count * n_sub + 1):
+                if i < count * n_sub:
+                    here = cols[i // n_sub]
+                    s, dp = scores(i % n_sub, kt_scr[:, here], vt_scr[:, here])
                 if held is not None:
-                    q = pl.ds((r - 1) * SUB, SUB)
+                    r = (i - 1) % n_sub
+                    there = cols[(i - 1) // n_sub]
+                    q = pl.ds(r * SUB, SUB)
                     p, ds = held
-                    av = jnp.dot(gt_scr[:, q], p, preferred_element_type=jnp.float32)
-                    ak = jnp.dot(qt_scr[:, q], ds, preferred_element_type=jnp.float32)
-                    acc_v = av if acc_v is None else acc_v + av
-                    acc_k = ak if acc_k is None else acc_k + ak
-                    dq = jnp.dot(ds, kk, preferred_element_type=jnp.float32)
-                    dqp[j, q, :] += dq
-                if r < n_sub:
-                    held = probs(r, s, dp, masked)
-            dv_scr[:, cols] += acc_v
-            dk_scr[:, cols] += acc_k
-
-        edge = lax.div(z, far) * (n_pref_last + j - (n_blocks - 1)) + n_blocks - 1
-
-        def step(b, carry):
-            block(b, False)
+                    av = jnp.dot(turned[j, 1, :, q], p, preferred_element_type=jnp.float32)
+                    ak = jnp.dot(turned[j, 0, :, q], ds, preferred_element_type=jnp.float32)
+                    acc_v = av if r == 0 else acc_v + av
+                    acc_k = ak if r == 0 else acc_k + ak
+                    dqp[j, q, :] += jnp.dot(ds, kv_scr[0, there, :], preferred_element_type=jnp.float32)
+                    if r == n_sub - 1:
+                        dv_scr[:, there] += acc_v
+                        dk_scr[:, there] += acc_k
+                if i < count * n_sub:
+                    held = probs(i % n_sub, s, dp, masked)
+
+        edge = lax.div(z, far) * (n_pref_last + j - n_blocks) + n_blocks
+        top = lax.min(high, edge)
+        many = lax.div(top - low, TOGETHER)
+        many = lax.max(many, 0)
+        mid = low + many * TOGETHER
+
+        def step(n, carry):
+            blocks(low + n * TOGETHER, TOGETHER)
             return carry
 
-        lax.fori_loop(low, lax.min(high, edge), step, 0)
+        lax.fori_loop(0, many, step, 0)
+
+        def single(b, carry):
+            blocks(b, 1)
+            return carry
+
+        lax.fori_loop(mid, top, single, 0)
 
         @pl.when((edge >= low) & (edge < high))
         def _():
-            block(edge, True)
+            blocks(edge, 1, True)
 
     dk_scr[...] = jnp.zeros_like(dk_scr)
     dv_scr[...] = jnp.zeros_like(dv_scr)
@@ -277,8 +300,10 @@
         vt_scr[:, cols] = kv_scr[1, cols, :].T
         return carry
 
-    kv_copy(0).wait()
-    kv_copy(1).wait_recv()
+    for copy in kv_copies(0):
+        copy.wait()
+    for copy in kv_copies(1):
+        copy.wait_recv()
     lax.fori_loop(own[0], own[1], turn, 0)
     wait_hop(st_hop, far)
 
@@ -324,7 +349,8 @@
         @pl.when(i == 2)
         def _():
             for s in range(2, n_cp):
-                kv_copy(s).wait_recv()
+                for copy in kv_copies(s):
+                    copy.wait_recv()
             lax.fori_loop(other[0], other[1], turn, 0)
 
         rs_service(
@@ -356,11 +382,13 @@
     for s in range(n_cp):
         whole = dqb.at[:, pl.ds(s * part, part), :]
         if s == 0:
-            pltpu.make_async_copy(whole, dq_out.at[c], dq_r.at[0]).wait()
+            pltpu.make_async_copy(whole, dq_out.at[:, c], dq_r.at[0]).wait()
         else:
-            remote(whole, dq_out.at[mate(s)], dq_s.at[s], dq_r.at[s], cp=mate(s)).wait()
-            remote(qg.at[mate(s)], gat.at[:, :, pl.ds(s * part, part), :], q_s.at[s], q_r.at[0, s], cp=mate(s)).wait_send()
-            kv_copy(s).wait_send()
+            remote(whole, dq_out.at[:, mate(s)], dq_s.at[s], dq_r.at[s], cp=mate(s)).wait()
+            for t, src in enumerate((q_in, g_in)):
+                remote(src.at[:, mate(s)], gat.at[:, t, pl.ds(s * part, part), :], q_s.at[s, t], q_r.at[0, s, t], cp=mate(s)).wait_send()
+            for copy in kv_copies(s):
+                copy.wait_send()
             st_copy(s).wait_send()
         for n, (acc, held, out, factor) in enumerate(pairs):
             home(held, out, s, n).wait()
@@ -382,6 +410,13 @@
                 d = 0 if up else 1
                 whole = dqp.at[:, slot(0), :]
                 remote(whole, whole, rs_s.at[d, h - 1], rs_r.at[d, 0, 0], cpo=z + 1 if up else z - 1).wait_send()
+
+
+def interleave_kernel(dk_ref, dv_ref, dk_out, dv_out):
+    heads, n, _ = dk_ref.shape
+    for src, dst in ((dk_ref, dk_out), (dv_ref, dv_out)):
+        for h in range(heads):
+            dst[pl.ds(h, n, stride=heads), :] = src[h]
 
 
 def solution(mesh):
@@ -408,16 +443,18 @@
         c = lax.axis_index('cp')
 
         delta = jnp.sum(grad_out.astype(f32) * attn_out.astype(f32), axis=-1)
-        st = jnp.stack([log_sum_exp, delta], axis=1).reshape(n_slices, 2, rows_dev, kv_heads, group)
-        st = st.transpose(3, 0, 1, 2, 4).reshape(kv_heads, n_slices * 2, part)
+        st = jnp.stack([log_sum_exp, delta], axis=1).transpose(3, 0, 1, 2).reshape(kv_heads, group, n_slices, 2, rows_dev)
+        st = st.transpose(0, 2, 3, 1, 4).reshape(kv_heads, n_slices * 2, part)
         st = jnp.pad(st, ((0, 0), (0, -(n_slices * 2) % 8), (0, 128 - part)))
-        qg = jnp.stack([queries, grad_out], axis=1).reshape(n_slices, 2, rows_dev, kv_heads, group, head_dim)
-        qg = jnp.transpose(qg, (3, 0, 1, 2, 4, 5)).reshape(kv_heads, n_slices, 2, part, head_dim)
-        kv = jnp.transpose(jnp.stack([key_cache, value_cache]), (2, 0, 1, 3))
+
+        def by_head(x):
+            return jnp.transpose(x, (0, 2, 1, 3)).reshape(n_slices, kv_heads, part, head_dim)
+
+        keys, values = (jnp.transpose(x, (1, 0, 2)) for x in (key_cache, value_cache))
 
         r = jnp.arange(rows)
         plane = (z - r // piece) % n_cpo
-        tok = plane * n_cp * rows_dev + (c ^ ((r % piece) // part)) * rows_dev + (r % part) // group
+        tok = plane * n_cp * rows_dev + (c ^ ((r % piece) // part)) * rows_dev + r % rows_dev
         tok = jnp.where(z == n_cpo - 1, tok, slice_len)
         qpos = jnp.broadcast_to(tok[:, None], (rows, 128)).astype(jnp.int32)
 
@@ -427,11 +464,11 @@
         dq, dk, dv = pl.pallas_call(
             functools.partial(attention_kernel, n_cpo, n_cp, n_pref_last, scale),
             out_shape=[
-                jax.ShapeDtypeStruct((kv_heads, n_slices, part, head_dim), bf),
+                jax.ShapeDtypeStruct((n_slices, kv_heads, part, head_dim), bf),
                 jax.ShapeDtypeStruct((kv_heads, key_rows, head_dim), f32),
                 jax.ShapeDtypeStruct((kv_heads, key_rows, head_dim), f32),
             ],
-            in_specs=[any_spec] * 3 + [vmem],
+            in_specs=[any_spec] * 5 + [vmem],
             out_specs=[any_spec] * 3,
             scratch_shapes=[
                 pltpu.VMEM((n_slices, 2, rows, head_dim), bf),
@@ -447,12 +484,11 @@
                 pltpu.VMEM((head_dim, plane_keys), f32),
                 pltpu.VMEM((plane_keys, head_dim), f32),
                 pltpu.VMEM((plane_keys, head_dim), f32),
-                pltpu.VMEM((head_dim, rows), bf),
-                pltpu.VMEM((head_dim, rows), bf),
+                pltpu.VMEM((n_slices, 2, head_dim, rows), bf),
                 pltpu.VMEM((rows, 128), f32),
                 pltpu.VMEM((rows, 128), f32),
-                dma((n_cp,)), dma((n_slices, n_cp)),
-                dma((n_cp,)), dma((n_cp,)),
+                dma((n_cp, 2)), dma((n_slices, n_cp, 2)),
+                dma((n_cp, 2)), dma((n_cp, 2)),
                 dma((n_cp,)), dma((n_cp,)),
                 dma((2, n_cpo - 1)), dma((n_cpo,)),
                 dma((2, n_cpo - 1)), dma((n_slices, n_cpo)),
@@ -462,10 +498,19 @@
             ],
             compiler_params=pltpu.CompilerParams(vmem_limit_bytes=63 * 1024 * 1024, collective_id=0, has_side_effects=True),
             name='attention_backward',
-        )(qg, kv, st, qpos)
-
-        dq = dq.reshape(kv_heads, n_slices, rows_dev, group, head_dim)
-        grad_query = jnp.transpose(dq, (1, 2, 0, 3, 4)).reshape(queries.shape)
-        return grad_query, jnp.transpose(dk, (1, 0, 2)), jnp.transpose(dv, (1, 0, 2))
+        )(by_head(queries), by_head(grad_out), keys, values, st, qpos)
+
+        block_rows = key_rows // 4
+        dk, dv = pl.pallas_call(
+            interleave_kernel,
+            grid=(4,),
+            out_shape=[jax.ShapeDtypeStruct((key_rows * kv_heads, head_dim), f32)] * 2,
+            in_specs=[pl.BlockSpec((kv_heads, block_rows, head_dim), lambda b: (0, b, 0))] * 2,
+            out_specs=[pl.BlockSpec((block_rows * kv_heads, head_dim), lambda b: (b, 0))] * 2,
+            compiler_params=pltpu.CompilerParams(vmem_limit_bytes=24 * 1024 * 1024),
+            name='interleave',
+        )(dk, dv)
+        grad_query = jnp.transpose(dq.reshape(n_slices, q_heads, rows_dev, head_dim), (0, 2, 1, 3))
+        return grad_query, dk.reshape(key_cache.shape), dv.reshape(key_cache.shape)
 
     return jax.shard_map(local_grads, mesh=mesh, in_specs=(row_spec, row_spec, row_spec, stat_spec, key_spec, key_spec), out_specs=(row_spec, key_spec, key_spec), check_vma=False)

time: 354 us -> 317 us (0.90)
  local copies, waits for them, and re-layouts: 24.5 us -> 8.36 us
  Pallas kernels: 320 us -> 306 us
  other arithmetic: 7.87 us -> 2.15 us
    pallas_call x1, Pallas kernels: 320 us -> 303 us  [local_grads(): pl.pallas_call(functools.partial(attention_kernel, n_cpo, n_cp, n_pref_la...]
    unnamed x17 -> x14, local copies, waits for them, and re-layouts: 13.3 us -> 4.5 us
    another operation x1 -> x0, other arithmetic: 4.05 us -> none  [local_grads(): jnp.stack([queries, grad_out], axis=1)]
    another operation x3 -> x0, local copies, waits for them, and re-layouts: 3.67 us -> none  [the longest x2 3.35 us: local_grads(): jnp.stack([queries, grad_out], axis=1)]
where the time goes in v3:
time: 317 us
  Pallas kernels  306 us (97%)
  local copies, waits for them, and re-layouts  8.36 us (3%)
    pallas_call x1, Pallas kernels, local_grads(): pl.pallas_call(functools.partial(attention_kernel, n_cpo, n_cp, n_pref_la...  303 us

profile of v3, /device:TPU:0, one launch (start us, length us, event | category | flops | bytes accessed | tf_op | source)
XLA Modules:
  0.0 317.0 jit_solution(13779023370842398000)
XLA Ops:
  0.6 0.0 copy-start.5
  0.7 2.1 multiply_reduce_fusion
  2.8 0.0 copy-done.5
  2.8 0.1 copy.18
  2.9 0.0 copy-start.3
  3.0 0.0 copy-start.2
  3.0 0.2 copy.19
  3.2 0.1 copy.20
  3.3 0.1 reshape.80
  3.4 0.6 pad.4.refs_4_
  4.0 1.1 broadcast_in_dim.11.refs_5_
  5.1 0.0 copy-done.3
  5.1 0.0 copy-done.2
  5.1 1.8 copy_bitcast_fusion
  6.9 302.7 %attention_backward.1 = (bf16[12,4,80,128]{3,2,1,0:T(8,128)(2,1)}, f32[4,1216,128]{2,1,0:T(8,128)}, f32[4,1216,128]{2,1,0:T(8,128)}) custom-call(bf16[12,4,80,128]{3,2,1,0:T(8,128)(2,1)} %bitcast.23, bf16[12,4,80,128]{3,2,1,0:T(8,128)(2,1)} %bitcast.22, bf16[4,1216,128]{2,1,0:T(8,128)(2,1)} %get-tuple-element.14.refs_2_, ...), custom_call_target="tpu_custom_call" | custom-call | tf_op jit(solution)/shard_map/attention_backward/pallas_call | solution.py:464
  309.6 0.0 copy-start
  309.6 1.7 copy-done
  311.3 0.0 copy-start.1
  311.3 1.7 copy-done.1
  313.0 0.0 copy-start.4
  313.0 3.1 interleave.1
  316.1 0.0 copy-done.4
  316.1 0.9 copy.24
  (2 shorter events, 0.1 us)
Async XLA Ops:
  0.6 2.1 copy-start.5
  2.9 2.2 copy-start.3
  3.0 2.1 copy-start.2
  309.6 1.7 copy-start
  311.3 1.7 copy-start.1
  313.0 3.1 copy-start.4
